TPU v7x, 32 devices: a whole 2x2x4 slice. The times are simulated.
32 devices in a mesh: gx: 8 (over y, x, core), gy: 4 (over z).
Axes of the slice: x: 2, y: 2, z: 4, core: 2. Of those that a mesh axis runs over, the one named last changes fastest.
Arguments:
- signals: float32 [16, 32, 16, 128], P('gx', 'gy'), may hold values from -6 to 6
- tiles: bfloat16 [16, 32, 4, 128, 128], P('gx', 'gy'), may hold values from 0 to 0.00390625
- tile_dir: int32 [16, 32, 4], P('gx', 'gy'), may hold values from 0 to 8
- tile_mask: int32 [16, 32, 4], P('gx', 'gy'), may hold values 0 or 1
- live_rows: int32 [16, 32], P('gx', 'gy'), may hold values from 32 to 128
- bound_rows: int32 [16, 32], P('gx', 'gy'), may hold values from 1 to 32, as said below
- scale_coeffs: float32 [6, 5], replicated, may hold values from -1 to 1
- spectral_bound: float32 [1], replicated, may hold values from 2.5 to 4
Outputs:
- coefficients: float32 [6, 16, 32, 16, 128], P(None, 'gx', 'gy')
- energy: float32 [6, 16], replicated
Inputs may be any that keep to these rules, and one draw needn't show every extreme that they name: `bound_rows`: in every draw, some blocks on every device have exactly 32 boundary rows.
All inputs are finite; a program needn't handle non-finite values. No bound on the sum of `tile_mask` on one device may be relied on, other than what follows from the above.
Results may differ from a plain program's by a relative error of at most 0.0003.
Values may be sent and summed in bfloat16 or wider, within the bound.
A program may use at most 64 MiB of HBM per device.

v0:
```python
import jax
import jax.numpy as jnp
from jax import lax
from jax.sharding import PartitionSpec as P

DEG = 4


def with_halo(array, sides, width):
    for axis, dim in sides:
        devices, length = (lax.axis_size(axis), array.shape[dim])
        up = [(i, (i + 1) % devices) for i in range(devices - 1)]
        down = [(j, i) for i, j in up]
        last = lax.slice_in_dim(array, length - width, length, axis=dim)
        first = lax.slice_in_dim(array, 0, width, axis=dim)
        before = lax.ppermute(last, axis, up)
        after = lax.ppermute(first, axis, down)
        array = jnp.concatenate([before, array, after], axis=dim)
    return array


def scaled_laplacian(values, adjacent, degree, factor):
    return factor * (degree * values - adjacent) - values


def shards(
    signals, tiles, tile_dir, tile_mask, live_rows, bound_rows, scale_coeffs, spectral_bound
):
    tile_size = signals.shape[3]
    extent_x = signals.shape[0]
    extent_y = signals.shape[1]
    slot_count = tiles.shape[2]
    block_count = extent_x * extent_y
    positions = lax.broadcasted_iota(jnp.int32, (1, 1, tile_size), 2)
    live_ind = (positions < live_rows[:, :, None]).astype(jnp.float32)
    bound_ind = (positions < bound_rows[:, :, None]).astype(jnp.float32)
    flat_tiles = tiles.reshape(block_count, slot_count, tile_size, tile_size)

    def adjacency(values):
        own_rows = values.astype(jnp.bfloat16)
        edge_rows = (values * bound_ind[:, :, None, :]).astype(jnp.bfloat16)
        padded = with_halo(edge_rows, (("gx", 0), ("gy", 1)), 1)
        slot_list = []
        for slot_index in range(slot_count):
            picked = jnp.zeros_like(own_rows)
            for direction in range(9):
                step_x = direction // 3 - 1
                step_y = direction % 3 - 1
                if direction == 4:
                    source = own_rows
                else:
                    source = padded[
                        1 + step_x : 1 + step_x + extent_x, 1 + step_y : 1 + step_y + extent_y
                    ]
                matches = (tile_dir[:, :, slot_index] == direction)[:, :, None, None]
                picked = jnp.where(matches, source, picked)
            kept = (tile_mask[:, :, slot_index] == 1)[:, :, None, None]
            picked = jnp.where(kept, picked, jnp.zeros_like(picked))
            slot_list.append(picked)
        inputs = jnp.stack(slot_list, axis=1 + 1)
        flat_inputs = inputs.reshape(block_count, slot_count, inputs.shape[3], tile_size)
        product = lax.dot_general(
            flat_inputs,
            flat_tiles,
            (((1, 3), (1, 3)), ((0,), (0,))),
            preferred_element_type=jnp.float32,
        )
        product = product.reshape(extent_x, extent_y, inputs.shape[3], tile_size)
        return product * live_ind[:, :, None, :]

    channels = signals.shape[2]
    initial = signals * live_ind[:, :, None, :]
    joined = jnp.concatenate([initial, live_ind[:, :, None, :]], axis=2)
    first_pass = adjacency(joined)
    degree = first_pass[:, :, channels:, :]
    factor = 2.0 / spectral_bound[0]
    previous = initial
    current = scaled_laplacian(initial, first_pass[:, :, :channels, :], degree, factor)
    totals = 0.5 * scale_coeffs[:, 0][:, None, None, None, None] * initial[None]
    totals = totals + scale_coeffs[:, 1][:, None, None, None, None] * current[None]
    for degree_index in range(2, DEG + 1):
        adjacent = adjacency(current)
        following = 2.0 * scaled_laplacian(current, adjacent, degree, factor) - previous
        previous = current
        current = following
        totals = totals + scale_coeffs[:, degree_index][:, None, None, None, None] * current[None]
    nodes = extent_x * extent_y * tile_size * lax.axis_size("gx") * lax.axis_size("gy")
    local_sums = jnp.sum(totals * totals, axis=(1, 2, 4))
    energy = lax.psum(local_sums, ("gx", "gy")) / nodes
    return (totals, energy)


def solution(mesh):
    placed = (
        P("gx", "gy", None, None),
        P("gx", "gy", None, None, None),
        P("gx", "gy", None),
        P("gx", "gy", None),
        P("gx", "gy"),
        P("gx", "gy"),
        P(),
        P(),
    )
    return jax.shard_map(
        shards,
        mesh=mesh,
        in_specs=placed,
        out_specs=(P(None, "gx", "gy", None, None), P()),
        check_vma=False,
    )
```

profile of v0, /device:TPU:0, one launch (start us, length us, event | category | flops | bytes accessed | tf_op | source)
XLA Modules:
  0.0 117.8 jit_solution(2510925606802948596)
XLA Ops:
  0.6 0.9 compare_convert_fusion
  1.6 0.8 fusion.35
  2.3 0.9 broadcast_multiply_fusion.1
  3.3 2.4 %collective-permute-start = (bf16[1,8,17,128]{3,2,1,0:T(8,128)(2,1)S(1)}, bf16[1,8,17,128]{3,2,1,0:T(8,128)(2,1)S(1)}, u32[]{:S(2)}, u32[]{:S(2)}) collective-permute-start(bf16[1,8,17,128]{3,2,1,0:T(8,128)(2,1)S(1)} %get-tuple-element.37), channel_id=1, source_target_pairs={{0,4},{4,8},{8,12},{12,16},{16,20},{20,24},{24,28},{1,5},{5,9},{9,... | collective-permute-start | bytes 104456 | tf_op jit(solution)/shard_map/ppermute | solution.py:16
  5.7 1.3 %collective-permute-start.1 = (bf16[1,8,17,128]{3,2,1,0:T(8,128)(2,1)S(1)}, bf16[1,8,17,128]{3,2,1,0:T(8,128)(2,1)S(1)}, u32[]{:S(2)}, u32[]{:S(2)}) collective-permute-start(bf16[1,8,17,128]{3,2,1,0:T(8,128)(2,1)S(1)} %get-tuple-element.38), channel_id=1, source_target_pairs={{4,0},{8,4},{12,8},{16,12},{20,16},{24,20},{28,24},{5,1},{9,5},{13... | collective-permute-start | bytes 104456 | tf_op jit(solution)/shard_map/ppermute | solution.py:17
  7.0 0.8 broadcast_compare_fusion.30
  7.8 0.8 broadcast_compare_fusion.31
  8.7 0.8 slice_compare_fusion.3
  9.8 1.1 collective-permute-done.1
  10.9 1.3 %collective-permute-start.2 = (bf16[4,1,17,128]{3,2,1,0:T(8,128)(2,1)S(1)}, bf16[4,1,17,128]{3,2,1,0:T(8,128)(2,1)S(1)}, u32[]{:S(2)}, u32[]{:S(2)}) collective-permute-start(bf16[4,1,17,128]{3,2,1,0:T(8,128)(2,1)S(1)} %get-tuple-element.23), channel_id=1, source_target_pairs={{1,0},{2,1},{3,2},{5,4},{6,5},{7,6},{9,8},{10,9},{11,10},{13,12},{... | collective-permute-start | bytes 52232 | tf_op jit(solution)/shard_map/ppermute | solution.py:17
  12.2 4.5 %collective-permute-start.3 = (bf16[4,1,17,128]{3,2,1,0:T(8,128)(2,1)S(1)}, bf16[4,1,17,128]{3,2,1,0:T(8,128)(2,1)S(1)}, u32[]{:S(2)}, u32[]{:S(2)}) collective-permute-start(bf16[4,1,17,128]{3,2,1,0:T(8,128)(2,1)S(1)} %get-tuple-element.24), channel_id=1, source_target_pairs={{0,1},{1,2},{2,3},{4,5},{5,6},{6,7},{8,9},{9,10},{10,11},{12,13},{... | collective-permute-start | bytes 52232 | tf_op jit(solution)/shard_map/ppermute | solution.py:16
  17.5 0.8 collective-permute-done.3
  20.2 3.6 %collective-permute-start.4 = (bf16[1,8,16,128]{3,2,1,0:T(8,128)(2,1)S(1)}, bf16[1,8,16,128]{3,2,1,0:T(8,128)(2,1)S(1)}, u32[]{:S(2)}, u32[]{:S(2)}) collective-permute-start(bf16[1,8,16,128]{3,2,1,0:T(8,128)(2,1)S(1)} %get-tuple-element.43), channel_id=1, source_target_pairs={{0,4},{4,8},{8,12},{12,16},{16,20},{20,24},{24,28},{1,5},{5,9},{9,... | collective-permute-start | bytes 98312 | tf_op jit(solution)/shard_map/ppermute | solution.py:16
  23.8 1.3 %collective-permute-start.5 = (bf16[1,8,16,128]{3,2,1,0:T(8,128)(2,1)S(1)}, bf16[1,8,16,128]{3,2,1,0:T(8,128)(2,1)S(1)}, u32[]{:S(2)}, u32[]{:S(2)}) collective-permute-start(bf16[1,8,16,128]{3,2,1,0:T(8,128)(2,1)S(1)} %get-tuple-element.44), channel_id=1, source_target_pairs={{4,0},{8,4},{12,8},{16,12},{20,16},{24,20},{28,24},{5,1},{9,5},{13... | collective-permute-start | bytes 98312 | tf_op jit(solution)/shard_map/ppermute | solution.py:17
  25.1 3.5 %collective-permute-done.5 = bf16[1,8,16,128]{3,2,1,0:T(8,128)(2,1)S(1)} collective-permute-done((bf16[1,8,16,128]{3,2,1,0:T(8,128)(2,1)S(1)}, bf16[1,8,16,128]{3,2,1,0:T(8,128)(2,1)S(1)}, u32[]{:S(2)}, u32[]{:S(2)}) %collective-permute-start.5) | collective-permute-done | bytes 32800 | tf_op jit(solution)/shard_map/ppermute | solution.py:17
  28.6 1.3 %collective-permute-start.6 = (bf16[4,1,16,128]{3,2,1,0:T(8,128)(2,1)S(1)}, bf16[4,1,16,128]{3,2,1,0:T(8,128)(2,1)S(1)}, u32[]{:S(2)}, u32[]{:S(2)}) collective-permute-start(bf16[4,1,16,128]{3,2,1,0:T(8,128)(2,1)S(1)} %get-tuple-element.35), channel_id=1, source_target_pairs={{1,0},{2,1},{3,2},{5,4},{6,5},{7,6},{9,8},{10,9},{11,10},{13,12},{... | collective-permute-start | bytes 49160 | tf_op jit(solution)/shard_map/ppermute | solution.py:17
  29.9 4.9 %collective-permute-start.7 = (bf16[4,1,16,128]{3,2,1,0:T(8,128)(2,1)S(1)}, bf16[4,1,16,128]{3,2,1,0:T(8,128)(2,1)S(1)}, u32[]{:S(2)}, u32[]{:S(2)}) collective-permute-start(bf16[4,1,16,128]{3,2,1,0:T(8,128)(2,1)S(1)} %get-tuple-element.36), channel_id=1, source_target_pairs={{0,1},{1,2},{2,3},{4,5},{5,6},{6,7},{8,9},{9,10},{10,11},{12,13},{... | collective-permute-start | bytes 49160 | tf_op jit(solution)/shard_map/ppermute | solution.py:16
  34.8 1.4 %collective-permute-done.7 = bf16[4,1,16,128]{3,2,1,0:T(8,128)(2,1)S(1)} collective-permute-done((bf16[4,1,16,128]{3,2,1,0:T(8,128)(2,1)S(1)}, bf16[4,1,16,128]{3,2,1,0:T(8,128)(2,1)S(1)}, u32[]{:S(2)}, u32[]{:S(2)}) %collective-permute-start.7) | collective-permute-done | bytes 16416 | tf_op jit(solution)/shard_map/ppermute | solution.py:16
  38.0 3.7 %collective-permute-start.8 = (bf16[1,8,16,128]{3,2,1,0:T(8,128)(2,1)S(1)}, bf16[1,8,16,128]{3,2,1,0:T(8,128)(2,1)S(1)}, u32[]{:S(2)}, u32[]{:S(2)}) collective-permute-start(bf16[1,8,16,128]{3,2,1,0:T(8,128)(2,1)S(1)} %get-tuple-element.41), channel_id=1, source_target_pairs={{0,4},{4,8},{8,12},{12,16},{16,20},{20,24},{24,28},{1,5},{5,9},{9,... | collective-permute-start | bytes 98312 | tf_op jit(solution)/shard_map/ppermute | solution.py:16
  41.7 1.3 %collective-permute-start.9 = (bf16[1,8,16,128]{3,2,1,0:T(8,128)(2,1)S(1)}, bf16[1,8,16,128]{3,2,1,0:T(8,128)(2,1)S(1)}, u32[]{:S(2)}, u32[]{:S(2)}) collective-permute-start(bf16[1,8,16,128]{3,2,1,0:T(8,128)(2,1)S(1)} %get-tuple-element.42), channel_id=1, source_target_pairs={{4,0},{8,4},{12,8},{16,12},{20,16},{24,20},{28,24},{5,1},{9,5},{13... | collective-permute-start | bytes 98312 | tf_op jit(solution)/shard_map/ppermute | solution.py:17
  43.0 2.2 %collective-permute-done.9 = bf16[1,8,16,128]{3,2,1,0:T(8,128)(2,1)S(1)} collective-permute-done((bf16[1,8,16,128]{3,2,1,0:T(8,128)(2,1)S(1)}, bf16[1,8,16,128]{3,2,1,0:T(8,128)(2,1)S(1)}, u32[]{:S(2)}, u32[]{:S(2)}) %collective-permute-start.9) | collective-permute-done | bytes 32800 | tf_op jit(solution)/shard_map/ppermute | solution.py:17
  45.2 1.3 %collective-permute-start.10 = (bf16[4,1,16,128]{3,2,1,0:T(8,128)(2,1)S(1)}, bf16[4,1,16,128]{3,2,1,0:T(8,128)(2,1)S(1)}, u32[]{:S(2)}, u32[]{:S(2)}) collective-permute-start(bf16[4,1,16,128]{3,2,1,0:T(8,128)(2,1)S(1)} %get-tuple-element.31), channel_id=1, source_target_pairs={{1,0},{2,1},{3,2},{5,4},{6,5},{7,6},{9,8},{10,9},{11,10},{13,12},{... | collective-permute-start | bytes 49160 | tf_op jit(solution)/shard_map/ppermute | solution.py:17
  46.4 4.8 %collective-permute-start.11 = (bf16[4,1,16,128]{3,2,1,0:T(8,128)(2,1)S(1)}, bf16[4,1,16,128]{3,2,1,0:T(8,128)(2,1)S(1)}, u32[]{:S(2)}, u32[]{:S(2)}) collective-permute-start(bf16[4,1,16,128]{3,2,1,0:T(8,128)(2,1)S(1)} %get-tuple-element.32), channel_id=1, source_target_pairs={{0,1},{1,2},{2,3},{4,5},{5,6},{6,7},{8,9},{9,10},{10,11},{12,13},{... | collective-permute-start | bytes 49160 | tf_op jit(solution)/shard_map/ppermute | solution.py:16
  51.3 1.4 %collective-permute-done.11 = bf16[4,1,16,128]{3,2,1,0:T(8,128)(2,1)S(1)} collective-permute-done((bf16[4,1,16,128]{3,2,1,0:T(8,128)(2,1)S(1)}, bf16[4,1,16,128]{3,2,1,0:T(8,128)(2,1)S(1)}, u32[]{:S(2)}, u32[]{:S(2)}) %collective-permute-start.11) | collective-permute-done | bytes 16416 | tf_op jit(solution)/shard_map/ppermute | solution.py:16
  54.5 4.1 %collective-permute-start.12 = (bf16[1,8,16,128]{3,2,1,0:T(8,128)(2,1)S(1)}, bf16[1,8,16,128]{3,2,1,0:T(8,128)(2,1)S(1)}, u32[]{:S(2)}, u32[]{:S(2)}) collective-permute-start(bf16[1,8,16,128]{3,2,1,0:T(8,128)(2,1)S(1)} %get-tuple-element.39), channel_id=1, source_target_pairs={{0,4},{4,8},{8,12},{12,16},{16,20},{20,24},{24,28},{1,5},{5,9},{9,... | collective-permute-start | bytes 98312 | tf_op jit(solution)/shard_map/ppermute | solution.py:16
  58.6 1.3 %collective-permute-start.13 = (bf16[1,8,16,128]{3,2,1,0:T(8,128)(2,1)S(1)}, bf16[1,8,16,128]{3,2,1,0:T(8,128)(2,1)S(1)}, u32[]{:S(2)}, u32[]{:S(2)}) collective-permute-start(bf16[1,8,16,128]{3,2,1,0:T(8,128)(2,1)S(1)} %get-tuple-element.40), channel_id=1, source_target_pairs={{4,0},{8,4},{12,8},{16,12},{20,16},{24,20},{28,24},{5,1},{9,5},{13... | collective-permute-start | bytes 98312 | tf_op jit(solution)/shard_map/ppermute | solution.py:17
  59.9 2.4 %collective-permute-done.13 = bf16[1,8,16,128]{3,2,1,0:T(8,128)(2,1)S(1)} collective-permute-done((bf16[1,8,16,128]{3,2,1,0:T(8,128)(2,1)S(1)}, bf16[1,8,16,128]{3,2,1,0:T(8,128)(2,1)S(1)}, u32[]{:S(2)}, u32[]{:S(2)}) %collective-permute-start.13) | collective-permute-done | bytes 32800 | tf_op jit(solution)/shard_map/ppermute | solution.py:17
  62.4 1.3 %collective-permute-start.14 = (bf16[4,1,16,128]{3,2,1,0:T(8,128)(2,1)S(1)}, bf16[4,1,16,128]{3,2,1,0:T(8,128)(2,1)S(1)}, u32[]{:S(2)}, u32[]{:S(2)}) collective-permute-start(bf16[4,1,16,128]{3,2,1,0:T(8,128)(2,1)S(1)} %get-tuple-element.27), channel_id=1, source_target_pairs={{1,0},{2,1},{3,2},{5,4},{6,5},{7,6},{9,8},{10,9},{11,10},{13,12},{... | collective-permute-start | bytes 49160 | tf_op jit(solution)/shard_map/ppermute | solution.py:17
  63.6 4.8 %collective-permute-start.15 = (bf16[4,1,16,128]{3,2,1,0:T(8,128)(2,1)S(1)}, bf16[4,1,16,128]{3,2,1,0:T(8,128)(2,1)S(1)}, u32[]{:S(2)}, u32[]{:S(2)}) collective-permute-start(bf16[4,1,16,128]{3,2,1,0:T(8,128)(2,1)S(1)} %get-tuple-element.28), channel_id=1, source_target_pairs={{0,1},{1,2},{2,3},{4,5},{5,6},{6,7},{8,9},{9,10},{10,11},{12,13},{... | collective-permute-start | bytes 49160 | tf_op jit(solution)/shard_map/ppermute | solution.py:16
  68.7 1.2 %collective-permute-done.15 = bf16[4,1,16,128]{3,2,1,0:T(8,128)(2,1)S(1)} collective-permute-done((bf16[4,1,16,128]{3,2,1,0:T(8,128)(2,1)S(1)}, bf16[4,1,16,128]{3,2,1,0:T(8,128)(2,1)S(1)}, u32[]{:S(2)}, u32[]{:S(2)}) %collective-permute-start.15) | collective-permute-done | bytes 16416 | tf_op jit(solution)/shard_map/ppermute | solution.py:16
  71.6 1.3 %multiply_reduce_fusion = (f32[6,16]{1,0:T(8,128)S(1)}, f32[6,2,8,16,128]{4,3,2,1,0:T(8,128)}) fusion(f32[2,8,16,128]{3,2,1,0:T(8,128)S(1)} %multiply_subtract_fusion, f32[6]{0:T(128)S(1)} %get-tuple-element.5, f32[2,8,16,128]{3,2,1,0:T(8,128)S(1)} %get-tuple-element.12, f32[6]{0:T(128)S(1)} %get-tuple-element.6, f32[2,8,16,128]{3,2,1,0:T(8,128)S(1)} %get-tuple-element.16, ...), kind=kLoop, calls=%fused_computation | loop fusion | flops 2162592 | bytes 1442296 | tf_op jit(solution)/shard_map/reduce_sum | solution.py:88
  72.9 44.3 %psum.7 = f32[6,16]{1,0:T(8,128)S(1)} all-reduce(f32[6,16]{1,0:T(8,128)S(1)} %get-tuple-element.7), channel_id=1, replica_groups=mesh['gx'=8,'gy'=4] {'gx','gy'}, use_global_device_ids=true, to_apply=%region_1.2 | all-reduce | flops 96 | bytes 768 | tf_op jit(solution)/shard_map/psum | solution.py:89
  (76 shorter events, 8.0 us)
Async XLA Ops:
  0.6 18.8 %copy-start = (bf16[2,8,4,128,128]{4,3,2,1,0:T(8,128)(2,1)S(1)}, bf16[2,8,4,128,128]{4,3,2,1,0:T(8,128)(2,1)}, u32[]{:S(2)}) copy-start(bf16[2,8,4,128,128]{4,3,2,1,0:T(8,128)(2,1)} %param.9) | copy-start | bytes 6291460
  3.3 6.5 %collective-permute-start = (bf16[1,8,17,128]{3,2,1,0:T(8,128)(2,1)S(1)}, bf16[1,8,17,128]{3,2,1,0:T(8,128)(2,1)S(1)}, u32[]{:S(2)}, u32[]{:S(2)}) collective-permute-start(bf16[1,8,17,128]{3,2,1,0:T(8,128)(2,1)S(1)} %get-tuple-element.37), channel_id=1, source_target_pairs={{0,4},{4,8},{8,12},{12,16},{16,20},{20,24},{24,28},{1,5},{5,9},{9,... | collective-permute-start | bytes 104456 | tf_op jit(solution)/shard_map/ppermute | solution.py:16
  5.7 5.2 %collective-permute-start.1 = (bf16[1,8,17,128]{3,2,1,0:T(8,128)(2,1)S(1)}, bf16[1,8,17,128]{3,2,1,0:T(8,128)(2,1)S(1)}, u32[]{:S(2)}, u32[]{:S(2)}) collective-permute-start(bf16[1,8,17,128]{3,2,1,0:T(8,128)(2,1)S(1)} %get-tuple-element.38), channel_id=1, source_target_pairs={{4,0},{8,4},{12,8},{16,12},{20,16},{24,20},{28,24},{5,1},{9,5},{13... | collective-permute-start | bytes 104456 | tf_op jit(solution)/shard_map/ppermute | solution.py:17
  10.9 6.6 %collective-permute-start.2 = (bf16[4,1,17,128]{3,2,1,0:T(8,128)(2,1)S(1)}, bf16[4,1,17,128]{3,2,1,0:T(8,128)(2,1)S(1)}, u32[]{:S(2)}, u32[]{:S(2)}) collective-permute-start(bf16[4,1,17,128]{3,2,1,0:T(8,128)(2,1)S(1)} %get-tuple-element.23), channel_id=1, source_target_pairs={{1,0},{2,1},{3,2},{5,4},{6,5},{7,6},{9,8},{10,9},{11,10},{13,12},{... | collective-permute-start | bytes 52232 | tf_op jit(solution)/shard_map/ppermute | solution.py:17
  12.2 6.1 %collective-permute-start.3 = (bf16[4,1,17,128]{3,2,1,0:T(8,128)(2,1)S(1)}, bf16[4,1,17,128]{3,2,1,0:T(8,128)(2,1)S(1)}, u32[]{:S(2)}, u32[]{:S(2)}) collective-permute-start(bf16[4,1,17,128]{3,2,1,0:T(8,128)(2,1)S(1)} %get-tuple-element.24), channel_id=1, source_target_pairs={{0,1},{1,2},{2,3},{4,5},{5,6},{6,7},{8,9},{9,10},{10,11},{12,13},{... | collective-permute-start | bytes 52232 | tf_op jit(solution)/shard_map/ppermute | solution.py:16
  19.2 1.0 copy-start.1
  20.2 4.9 %collective-permute-start.4 = (bf16[1,8,16,128]{3,2,1,0:T(8,128)(2,1)S(1)}, bf16[1,8,16,128]{3,2,1,0:T(8,128)(2,1)S(1)}, u32[]{:S(2)}, u32[]{:S(2)}) collective-permute-start(bf16[1,8,16,128]{3,2,1,0:T(8,128)(2,1)S(1)} %get-tuple-element.43), channel_id=1, source_target_pairs={{0,4},{4,8},{8,12},{12,16},{16,20},{20,24},{24,28},{1,5},{5,9},{9,... | collective-permute-start | bytes 98312 | tf_op jit(solution)/shard_map/ppermute | solution.py:16
  23.8 4.8 %collective-permute-start.5 = (bf16[1,8,16,128]{3,2,1,0:T(8,128)(2,1)S(1)}, bf16[1,8,16,128]{3,2,1,0:T(8,128)(2,1)S(1)}, u32[]{:S(2)}, u32[]{:S(2)}) collective-permute-start(bf16[1,8,16,128]{3,2,1,0:T(8,128)(2,1)S(1)} %get-tuple-element.44), channel_id=1, source_target_pairs={{4,0},{8,4},{12,8},{16,12},{20,16},{24,20},{28,24},{5,1},{9,5},{13... | collective-permute-start | bytes 98312 | tf_op jit(solution)/shard_map/ppermute | solution.py:17
  28.6 6.2 %collective-permute-start.6 = (bf16[4,1,16,128]{3,2,1,0:T(8,128)(2,1)S(1)}, bf16[4,1,16,128]{3,2,1,0:T(8,128)(2,1)S(1)}, u32[]{:S(2)}, u32[]{:S(2)}) collective-permute-start(bf16[4,1,16,128]{3,2,1,0:T(8,128)(2,1)S(1)} %get-tuple-element.35), channel_id=1, source_target_pairs={{1,0},{2,1},{3,2},{5,4},{6,5},{7,6},{9,8},{10,9},{11,10},{13,12},{... | collective-permute-start | bytes 49160 | tf_op jit(solution)/shard_map/ppermute | solution.py:17
  29.9 6.3 %collective-permute-start.7 = (bf16[4,1,16,128]{3,2,1,0:T(8,128)(2,1)S(1)}, bf16[4,1,16,128]{3,2,1,0:T(8,128)(2,1)S(1)}, u32[]{:S(2)}, u32[]{:S(2)}) collective-permute-start(bf16[4,1,16,128]{3,2,1,0:T(8,128)(2,1)S(1)} %get-tuple-element.36), channel_id=1, source_target_pairs={{0,1},{1,2},{2,3},{4,5},{5,6},{6,7},{8,9},{9,10},{10,11},{12,13},{... | collective-permute-start | bytes 49160 | tf_op jit(solution)/shard_map/ppermute | solution.py:16
  38.0 5.0 %collective-permute-start.8 = (bf16[1,8,16,128]{3,2,1,0:T(8,128)(2,1)S(1)}, bf16[1,8,16,128]{3,2,1,0:T(8,128)(2,1)S(1)}, u32[]{:S(2)}, u32[]{:S(2)}) collective-permute-start(bf16[1,8,16,128]{3,2,1,0:T(8,128)(2,1)S(1)} %get-tuple-element.41), channel_id=1, source_target_pairs={{0,4},{4,8},{8,12},{12,16},{16,20},{20,24},{24,28},{1,5},{5,9},{9,... | collective-permute-start | bytes 98312 | tf_op jit(solution)/shard_map/ppermute | solution.py:16
  41.7 3.5 %collective-permute-start.9 = (bf16[1,8,16,128]{3,2,1,0:T(8,128)(2,1)S(1)}, bf16[1,8,16,128]{3,2,1,0:T(8,128)(2,1)S(1)}, u32[]{:S(2)}, u32[]{:S(2)}) collective-permute-start(bf16[1,8,16,128]{3,2,1,0:T(8,128)(2,1)S(1)} %get-tuple-element.42), channel_id=1, source_target_pairs={{4,0},{8,4},{12,8},{16,12},{20,16},{24,20},{28,24},{5,1},{9,5},{13... | collective-permute-start | bytes 98312 | tf_op jit(solution)/shard_map/ppermute | solution.py:17
  45.2 6.1 %collective-permute-start.10 = (bf16[4,1,16,128]{3,2,1,0:T(8,128)(2,1)S(1)}, bf16[4,1,16,128]{3,2,1,0:T(8,128)(2,1)S(1)}, u32[]{:S(2)}, u32[]{:S(2)}) collective-permute-start(bf16[4,1,16,128]{3,2,1,0:T(8,128)(2,1)S(1)} %get-tuple-element.31), channel_id=1, source_target_pairs={{1,0},{2,1},{3,2},{5,4},{6,5},{7,6},{9,8},{10,9},{11,10},{13,12},{... | collective-permute-start | bytes 49160 | tf_op jit(solution)/shard_map/ppermute | solution.py:17
  46.4 6.3 %collective-permute-start.11 = (bf16[4,1,16,128]{3,2,1,0:T(8,128)(2,1)S(1)}, bf16[4,1,16,128]{3,2,1,0:T(8,128)(2,1)S(1)}, u32[]{:S(2)}, u32[]{:S(2)}) collective-permute-start(bf16[4,1,16,128]{3,2,1,0:T(8,128)(2,1)S(1)} %get-tuple-element.32), channel_id=1, source_target_pairs={{0,1},{1,2},{2,3},{4,5},{5,6},{6,7},{8,9},{9,10},{10,11},{12,13},{... | collective-permute-start | bytes 49160 | tf_op jit(solution)/shard_map/ppermute | solution.py:16
  53.5 15.0 %copy-start.2 = (f32[6,5]{1,0:T(8,128)S(1)}, f32[6,5]{1,0:T(8,128)}, u32[]{:S(2)}) copy-start(f32[6,5]{1,0:T(8,128)} %param.14) | copy-start | bytes 364
  54.5 5.4 %collective-permute-start.12 = (bf16[1,8,16,128]{3,2,1,0:T(8,128)(2,1)S(1)}, bf16[1,8,16,128]{3,2,1,0:T(8,128)(2,1)S(1)}, u32[]{:S(2)}, u32[]{:S(2)}) collective-permute-start(bf16[1,8,16,128]{3,2,1,0:T(8,128)(2,1)S(1)} %get-tuple-element.39), channel_id=1, source_target_pairs={{0,4},{4,8},{8,12},{12,16},{16,20},{20,24},{24,28},{1,5},{5,9},{9,... | collective-permute-start | bytes 98312 | tf_op jit(solution)/shard_map/ppermute | solution.py:16
  58.6 3.7 %collective-permute-start.13 = (bf16[1,8,16,128]{3,2,1,0:T(8,128)(2,1)S(1)}, bf16[1,8,16,128]{3,2,1,0:T(8,128)(2,1)S(1)}, u32[]{:S(2)}, u32[]{:S(2)}) collective-permute-start(bf16[1,8,16,128]{3,2,1,0:T(8,128)(2,1)S(1)} %get-tuple-element.40), channel_id=1, source_target_pairs={{4,0},{8,4},{12,8},{16,12},{20,16},{24,20},{28,24},{5,1},{9,5},{13... | collective-permute-start | bytes 98312 | tf_op jit(solution)/shard_map/ppermute | solution.py:17
  62.4 6.4 %collective-permute-start.14 = (bf16[4,1,16,128]{3,2,1,0:T(8,128)(2,1)S(1)}, bf16[4,1,16,128]{3,2,1,0:T(8,128)(2,1)S(1)}, u32[]{:S(2)}, u32[]{:S(2)}) collective-permute-start(bf16[4,1,16,128]{3,2,1,0:T(8,128)(2,1)S(1)} %get-tuple-element.27), channel_id=1, source_target_pairs={{1,0},{2,1},{3,2},{5,4},{6,5},{7,6},{9,8},{10,9},{11,10},{13,12},{... | collective-permute-start | bytes 49160 | tf_op jit(solution)/shard_map/ppermute | solution.py:17
  63.6 6.3 %collective-permute-start.15 = (bf16[4,1,16,128]{3,2,1,0:T(8,128)(2,1)S(1)}, bf16[4,1,16,128]{3,2,1,0:T(8,128)(2,1)S(1)}, u32[]{:S(2)}, u32[]{:S(2)}) collective-permute-start(bf16[4,1,16,128]{3,2,1,0:T(8,128)(2,1)S(1)} %get-tuple-element.28), channel_id=1, source_target_pairs={{0,1},{1,2},{2,3},{4,5},{5,6},{6,7},{8,9},{9,10},{10,11},{12,13},{... | collective-permute-start | bytes 49160 | tf_op jit(solution)/shard_map/ppermute | solution.py:16
where the time goes:
time: 119 us; the launch traced here: 118 us
  blocking collectives  44.3 us (37%)
  starting transfers between devices  43.2 us (36%)
  waiting for transfers between devices  14 us (12%)
  other arithmetic  11.6 us (10%)
  matrix products  2.6 us (2%)
  between operations  1.96 us (2%)
    psum x1, blocking collectives, shards(): energy = lax.psum(local_sums, ('gx', 'gy')) / nodes  44.3 us
    ppermute x8, starting transfers between devices, with_halo(): before = lax.ppermute(last, axis, up)  32.9 us
    ppermute x8, starting transfers between devices, with_halo(): after = lax.ppermute(first, axis, down)  10.3 us
    ppermute x8, waiting for transfers between devices, with_halo(): after = lax.ppermute(first, axis, down)  9.19 us
    ppermute x8, waiting for transfers between devices, with_halo(): before = lax.ppermute(last, axis, up)  4.79 us
    select_n x16, other arithmetic, adjacency(): picked = jnp.where(kept, picked, jnp.zeros_like(picked))  3.91 us
    dot_general x4, matrix products, adjacency(): lax.dot_general(flat_inputs, flat_tiles, (((1, 3), (1, 3)), ((0,), (0,)))...  2.6 us
  transfers between devices with their start and end apart: 16, of which 8 were waited for; matrix products, arithmetic and copies ran while one was open for 2% of the time, Pallas kernels for 0%

commit v1 on v0

--- a/solution.py
+++ b/solution.py
@@ -1,9 +1,19 @@
+import functools
 import jax
 import jax.numpy as jnp
 from jax import lax
 from jax.sharding import PartitionSpec as P
+from jax.lax import psum
 
 DEG = 4
+
+
+def perform_tiles_now(array_in, device_axis, named_axis):
+    long_array = psum(psum(array_in, axis_name=device_axis), axis_name=named_axis)
+    return long_array
+
+
+track_copies = functools.partial(perform_tiles_now, device_axis="gy", named_axis="gx")
 
 
 def with_halo(array, sides, width):
@@ -86,7 +96,7 @@
         totals = totals + scale_coeffs[:, degree_index][:, None, None, None, None] * current[None]
     nodes = extent_x * extent_y * tile_size * lax.axis_size("gx") * lax.axis_size("gy")
     local_sums = jnp.sum(totals * totals, axis=(1, 2, 4))
-    energy = lax.psum(local_sums, ("gx", "gy")) / nodes
+    energy = track_copies(local_sums) / nodes
     return (totals, energy)
 
 

time: 119 us -> 102 us (0.86)
  the two profiles are of different devices: /device:TPU:0 before, /device:TPU:5 now
where the time goes in v1:
time: 102 us; the launch traced here: 101 us
  starting transfers between devices  46.1 us (45%)
  blocking collectives  27.8 us (27%)
  other arithmetic  11.6 us (11%)
  waiting for transfers between devices  11 us (11%)
  matrix products  2.6 us (3%)
  between operations  1.97 us (2%)
    ppermute x8, starting transfers between devices, with_halo(): before = lax.ppermute(last, axis, up)  31 us
    psum x1, blocking collectives, perform_tiles_now(): psum(psum(array_in, axis_name=device_axis), axis_name=named_axis)  16.9 us
    ppermute x8, starting transfers between devices, with_halo(): after = lax.ppermute(first, axis, down)  15.1 us
    psum x1, blocking collectives, perform_tiles_now(): psum(array_in, axis_name=device_axis)  10.9 us
    ppermute x8, waiting for transfers between devices, with_halo(): after = lax.ppermute(first, axis, down)  8.47 us
    select_n x16, other arithmetic, adjacency(): picked = jnp.where(kept, picked, jnp.zeros_like(picked))  3.91 us
    dot_general x4, matrix products, adjacency(): lax.dot_general(flat_inputs, flat_tiles, (((1, 3), (1, 3)), ((0,), (0,)))...  2.6 us
    ppermute x8, waiting for transfers between devices, with_halo(): before = lax.ppermute(last, axis, up)  2.49 us
  transfers between devices with their start and end apart: 16, of which 8 were waited for; matrix products, arithmetic and copies ran while one was open for 3% of the time, Pallas kernels for 0%

profile of v1, /device:TPU:5, one launch (start us, length us, event | category | flops | bytes accessed | tf_op | source)
XLA Modules:
  0.0 101.2 jit_solution(18064448871456457632)
XLA Ops:
  0.6 0.9 compare_convert_fusion
  1.6 0.8 fusion.35
  2.3 0.9 broadcast_multiply_fusion.1
  3.3 3.7 %collective-permute-start = (bf16[1,8,17,128]{3,2,1,0:T(8,128)(2,1)S(1)}, bf16[1,8,17,128]{3,2,1,0:T(8,128)(2,1)S(1)}, u32[]{:S(2)}, u32[]{:S(2)}) collective-permute-start(bf16[1,8,17,128]{3,2,1,0:T(8,128)(2,1)S(1)} %get-tuple-element.37), channel_id=1, source_target_pairs={{0,4},{4,8},{8,12},{12,16},{16,20},{20,24},{24,28},{1,5},{5,9},{9,... | collective-permute-start | bytes 104456 | tf_op jit(solution)/shard_map/ppermute | solution.py:26
  7.0 1.9 %collective-permute-start.1 = (bf16[1,8,17,128]{3,2,1,0:T(8,128)(2,1)S(1)}, bf16[1,8,17,128]{3,2,1,0:T(8,128)(2,1)S(1)}, u32[]{:S(2)}, u32[]{:S(2)}) collective-permute-start(bf16[1,8,17,128]{3,2,1,0:T(8,128)(2,1)S(1)} %get-tuple-element.38), channel_id=1, source_target_pairs={{4,0},{8,4},{12,8},{16,12},{20,16},{24,20},{28,24},{5,1},{9,5},{13... | collective-permute-start | bytes 104456 | tf_op jit(solution)/shard_map/ppermute | solution.py:27
  8.9 0.8 broadcast_compare_fusion.30
  9.8 0.8 broadcast_compare_fusion.31
  10.6 0.8 slice_compare_fusion.3
  11.7 0.7 collective-permute-done.1
  12.4 1.3 %collective-permute-start.2 = (bf16[4,1,17,128]{3,2,1,0:T(8,128)(2,1)S(1)}, bf16[4,1,17,128]{3,2,1,0:T(8,128)(2,1)S(1)}, u32[]{:S(2)}, u32[]{:S(2)}) collective-permute-start(bf16[4,1,17,128]{3,2,1,0:T(8,128)(2,1)S(1)} %get-tuple-element.23), channel_id=1, source_target_pairs={{1,0},{2,1},{3,2},{5,4},{6,5},{7,6},{9,8},{10,9},{11,10},{13,12},{... | collective-permute-start | bytes 52232 | tf_op jit(solution)/shard_map/ppermute | solution.py:27
  13.7 4.0 %collective-permute-start.3 = (bf16[4,1,17,128]{3,2,1,0:T(8,128)(2,1)S(1)}, bf16[4,1,17,128]{3,2,1,0:T(8,128)(2,1)S(1)}, u32[]{:S(2)}, u32[]{:S(2)}) collective-permute-start(bf16[4,1,17,128]{3,2,1,0:T(8,128)(2,1)S(1)} %get-tuple-element.24), channel_id=1, source_target_pairs={{0,1},{1,2},{2,3},{4,5},{5,6},{6,7},{8,9},{9,10},{10,11},{12,13},{... | collective-permute-start | bytes 52232 | tf_op jit(solution)/shard_map/ppermute | solution.py:26
  19.8 0.7 fusion
  20.6 4.1 %collective-permute-start.4 = (bf16[1,8,16,128]{3,2,1,0:T(8,128)(2,1)S(1)}, bf16[1,8,16,128]{3,2,1,0:T(8,128)(2,1)S(1)}, u32[]{:S(2)}, u32[]{:S(2)}) collective-permute-start(bf16[1,8,16,128]{3,2,1,0:T(8,128)(2,1)S(1)} %get-tuple-element.43), channel_id=1, source_target_pairs={{0,4},{4,8},{8,12},{12,16},{16,20},{20,24},{24,28},{1,5},{5,9},{9,... | collective-permute-start | bytes 98312 | tf_op jit(solution)/shard_map/ppermute | solution.py:26
  24.7 1.9 %collective-permute-start.5 = (bf16[1,8,16,128]{3,2,1,0:T(8,128)(2,1)S(1)}, bf16[1,8,16,128]{3,2,1,0:T(8,128)(2,1)S(1)}, u32[]{:S(2)}, u32[]{:S(2)}) collective-permute-start(bf16[1,8,16,128]{3,2,1,0:T(8,128)(2,1)S(1)} %get-tuple-element.44), channel_id=1, source_target_pairs={{4,0},{8,4},{12,8},{16,12},{20,16},{24,20},{28,24},{5,1},{9,5},{13... | collective-permute-start | bytes 98312 | tf_op jit(solution)/shard_map/ppermute | solution.py:27
  26.6 3.3 %collective-permute-done.5 = bf16[1,8,16,128]{3,2,1,0:T(8,128)(2,1)S(1)} collective-permute-done((bf16[1,8,16,128]{3,2,1,0:T(8,128)(2,1)S(1)}, bf16[1,8,16,128]{3,2,1,0:T(8,128)(2,1)S(1)}, u32[]{:S(2)}, u32[]{:S(2)}) %collective-permute-start.5) | collective-permute-done | bytes 32800 | tf_op jit(solution)/shard_map/ppermute | solution.py:27
  29.9 1.3 %collective-permute-start.6 = (bf16[4,1,16,128]{3,2,1,0:T(8,128)(2,1)S(1)}, bf16[4,1,16,128]{3,2,1,0:T(8,128)(2,1)S(1)}, u32[]{:S(2)}, u32[]{:S(2)}) collective-permute-start(bf16[4,1,16,128]{3,2,1,0:T(8,128)(2,1)S(1)} %get-tuple-element.35), channel_id=1, source_target_pairs={{1,0},{2,1},{3,2},{5,4},{6,5},{7,6},{9,8},{10,9},{11,10},{13,12},{... | collective-permute-start | bytes 49160 | tf_op jit(solution)/shard_map/ppermute | solution.py:27
  31.2 4.6 %collective-permute-start.7 = (bf16[4,1,16,128]{3,2,1,0:T(8,128)(2,1)S(1)}, bf16[4,1,16,128]{3,2,1,0:T(8,128)(2,1)S(1)}, u32[]{:S(2)}, u32[]{:S(2)}) collective-permute-start(bf16[4,1,16,128]{3,2,1,0:T(8,128)(2,1)S(1)} %get-tuple-element.36), channel_id=1, source_target_pairs={{0,1},{1,2},{2,3},{4,5},{5,6},{6,7},{8,9},{9,10},{10,11},{12,13},{... | collective-permute-start | bytes 49160 | tf_op jit(solution)/shard_map/ppermute | solution.py:26
  35.8 0.8 collective-permute-done.7
  38.4 2.8 %collective-permute-start.8 = (bf16[1,8,16,128]{3,2,1,0:T(8,128)(2,1)S(1)}, bf16[1,8,16,128]{3,2,1,0:T(8,128)(2,1)S(1)}, u32[]{:S(2)}, u32[]{:S(2)}) collective-permute-start(bf16[1,8,16,128]{3,2,1,0:T(8,128)(2,1)S(1)} %get-tuple-element.41), channel_id=1, source_target_pairs={{0,4},{4,8},{8,12},{12,16},{16,20},{20,24},{24,28},{1,5},{5,9},{9,... | collective-permute-start | bytes 98312 | tf_op jit(solution)/shard_map/ppermute | solution.py:26
  41.2 2.6 %collective-permute-start.9 = (bf16[1,8,16,128]{3,2,1,0:T(8,128)(2,1)S(1)}, bf16[1,8,16,128]{3,2,1,0:T(8,128)(2,1)S(1)}, u32[]{:S(2)}, u32[]{:S(2)}) collective-permute-start(bf16[1,8,16,128]{3,2,1,0:T(8,128)(2,1)S(1)} %get-tuple-element.42), channel_id=1, source_target_pairs={{4,0},{8,4},{12,8},{16,12},{20,16},{24,20},{28,24},{5,1},{9,5},{13... | collective-permute-start | bytes 98312 | tf_op jit(solution)/shard_map/ppermute | solution.py:27
  43.8 2.6 %collective-permute-done.9 = bf16[1,8,16,128]{3,2,1,0:T(8,128)(2,1)S(1)} collective-permute-done((bf16[1,8,16,128]{3,2,1,0:T(8,128)(2,1)S(1)}, bf16[1,8,16,128]{3,2,1,0:T(8,128)(2,1)S(1)}, u32[]{:S(2)}, u32[]{:S(2)}) %collective-permute-start.9) | collective-permute-done | bytes 32800 | tf_op jit(solution)/shard_map/ppermute | solution.py:27
  46.4 1.3 %collective-permute-start.10 = (bf16[4,1,16,128]{3,2,1,0:T(8,128)(2,1)S(1)}, bf16[4,1,16,128]{3,2,1,0:T(8,128)(2,1)S(1)}, u32[]{:S(2)}, u32[]{:S(2)}) collective-permute-start(bf16[4,1,16,128]{3,2,1,0:T(8,128)(2,1)S(1)} %get-tuple-element.31), channel_id=1, source_target_pairs={{1,0},{2,1},{3,2},{5,4},{6,5},{7,6},{9,8},{10,9},{11,10},{13,12},{... | collective-permute-start | bytes 49160 | tf_op jit(solution)/shard_map/ppermute | solution.py:27
  47.7 4.5 %collective-permute-start.11 = (bf16[4,1,16,128]{3,2,1,0:T(8,128)(2,1)S(1)}, bf16[4,1,16,128]{3,2,1,0:T(8,128)(2,1)S(1)}, u32[]{:S(2)}, u32[]{:S(2)}) collective-permute-start(bf16[4,1,16,128]{3,2,1,0:T(8,128)(2,1)S(1)} %get-tuple-element.32), channel_id=1, source_target_pairs={{0,1},{1,2},{2,3},{4,5},{5,6},{6,7},{8,9},{9,10},{10,11},{12,13},{... | collective-permute-start | bytes 49160 | tf_op jit(solution)/shard_map/ppermute | solution.py:26
  52.3 0.8 collective-permute-done.11
  54.9 2.8 %collective-permute-start.12 = (bf16[1,8,16,128]{3,2,1,0:T(8,128)(2,1)S(1)}, bf16[1,8,16,128]{3,2,1,0:T(8,128)(2,1)S(1)}, u32[]{:S(2)}, u32[]{:S(2)}) collective-permute-start(bf16[1,8,16,128]{3,2,1,0:T(8,128)(2,1)S(1)} %get-tuple-element.39), channel_id=1, source_target_pairs={{0,4},{4,8},{8,12},{12,16},{16,20},{20,24},{24,28},{1,5},{5,9},{9,... | collective-permute-start | bytes 98312 | tf_op jit(solution)/shard_map/ppermute | solution.py:26
  57.7 3.5 %collective-permute-start.13 = (bf16[1,8,16,128]{3,2,1,0:T(8,128)(2,1)S(1)}, bf16[1,8,16,128]{3,2,1,0:T(8,128)(2,1)S(1)}, u32[]{:S(2)}, u32[]{:S(2)}) collective-permute-start(bf16[1,8,16,128]{3,2,1,0:T(8,128)(2,1)S(1)} %get-tuple-element.40), channel_id=1, source_target_pairs={{4,0},{8,4},{12,8},{16,12},{20,16},{24,20},{28,24},{5,1},{9,5},{13... | collective-permute-start | bytes 98312 | tf_op jit(solution)/shard_map/ppermute | solution.py:27
  61.2 1.9 %collective-permute-done.13 = bf16[1,8,16,128]{3,2,1,0:T(8,128)(2,1)S(1)} collective-permute-done((bf16[1,8,16,128]{3,2,1,0:T(8,128)(2,1)S(1)}, bf16[1,8,16,128]{3,2,1,0:T(8,128)(2,1)S(1)}, u32[]{:S(2)}, u32[]{:S(2)}) %collective-permute-start.13) | collective-permute-done | bytes 32800 | tf_op jit(solution)/shard_map/ppermute | solution.py:27
  63.1 1.3 %collective-permute-start.14 = (bf16[4,1,16,128]{3,2,1,0:T(8,128)(2,1)S(1)}, bf16[4,1,16,128]{3,2,1,0:T(8,128)(2,1)S(1)}, u32[]{:S(2)}, u32[]{:S(2)}) collective-permute-start(bf16[4,1,16,128]{3,2,1,0:T(8,128)(2,1)S(1)} %get-tuple-element.27), channel_id=1, source_target_pairs={{1,0},{2,1},{3,2},{5,4},{6,5},{7,6},{9,8},{10,9},{11,10},{13,12},{... | collective-permute-start | bytes 49160 | tf_op jit(solution)/shard_map/ppermute | solution.py:27
  64.4 4.5 %collective-permute-start.15 = (bf16[4,1,16,128]{3,2,1,0:T(8,128)(2,1)S(1)}, bf16[4,1,16,128]{3,2,1,0:T(8,128)(2,1)S(1)}, u32[]{:S(2)}, u32[]{:S(2)}) collective-permute-start(bf16[4,1,16,128]{3,2,1,0:T(8,128)(2,1)S(1)} %get-tuple-element.28), channel_id=1, source_target_pairs={{0,1},{1,2},{2,3},{4,5},{5,6},{6,7},{8,9},{9,10},{10,11},{12,13},{... | collective-permute-start | bytes 49160 | tf_op jit(solution)/shard_map/ppermute | solution.py:26
  71.5 1.3 %multiply_reduce_fusion = (f32[6,16]{1,0:T(8,128)S(1)}, f32[6,2,8,16,128]{4,3,2,1,0:T(8,128)}) fusion(f32[2,8,16,128]{3,2,1,0:T(8,128)S(1)} %multiply_subtract_fusion, f32[6]{0:T(128)S(1)} %get-tuple-element.5, f32[2,8,16,128]{3,2,1,0:T(8,128)S(1)} %get-tuple-element.12, f32[6]{0:T(128)S(1)} %get-tuple-element.6, f32[2,8,16,128]{3,2,1,0:T(8,128)S(1)} %get-tuple-element.16, ...), kind=kLoop, calls=%fused_computation | loop fusion | flops 2162592 | bytes 1442296 | tf_op jit(solution)/shard_map/reduce_sum | solution.py:98
  72.8 10.9 %psum.14 = f32[6,16]{1,0:T(8,128)S(1)} all-reduce(f32[6,16]{1,0:T(8,128)S(1)} %get-tuple-element.7), channel_id=1, replica_groups=mesh['gx'=8,'gy'=4] {'gy'}, use_global_device_ids=true, to_apply=%region_1.2 | all-reduce | flops 96 | bytes 768 | tf_op jit(solution)/shard_map/psum | solution.py:12
  83.7 16.9 %psum.15 = f32[6,16]{1,0:T(8,128)S(1)} all-reduce(f32[6,16]{1,0:T(8,128)S(1)} %psum.14), channel_id=1, replica_groups=mesh['gx'=8,'gy'=4] {'gx'}, use_global_device_ids=true, to_apply=%region_2.3 | all-reduce | flops 96 | bytes 768 | tf_op jit(solution)/shard_map/psum | solution.py:12
  (77 shorter events, 8.2 us)
Async XLA Ops:
  0.6 19.1 %copy-start = (bf16[2,8,4,128,128]{4,3,2,1,0:T(8,128)(2,1)S(1)}, bf16[2,8,4,128,128]{4,3,2,1,0:T(8,128)(2,1)}, u32[]{:S(2)}) copy-start(bf16[2,8,4,128,128]{4,3,2,1,0:T(8,128)(2,1)} %param.9) | copy-start | bytes 6291460
  3.3 8.4 %collective-permute-start = (bf16[1,8,17,128]{3,2,1,0:T(8,128)(2,1)S(1)}, bf16[1,8,17,128]{3,2,1,0:T(8,128)(2,1)S(1)}, u32[]{:S(2)}, u32[]{:S(2)}) collective-permute-start(bf16[1,8,17,128]{3,2,1,0:T(8,128)(2,1)S(1)} %get-tuple-element.37), channel_id=1, source_target_pairs={{0,4},{4,8},{8,12},{12,16},{16,20},{20,24},{24,28},{1,5},{5,9},{9,... | collective-permute-start | bytes 104456 | tf_op jit(solution)/shard_map/ppermute | solution.py:26
  7.0 5.4 %collective-permute-start.1 = (bf16[1,8,17,128]{3,2,1,0:T(8,128)(2,1)S(1)}, bf16[1,8,17,128]{3,2,1,0:T(8,128)(2,1)S(1)}, u32[]{:S(2)}, u32[]{:S(2)}) collective-permute-start(bf16[1,8,17,128]{3,2,1,0:T(8,128)(2,1)S(1)} %get-tuple-element.38), channel_id=1, source_target_pairs={{4,0},{8,4},{12,8},{16,12},{20,16},{24,20},{28,24},{5,1},{9,5},{13... | collective-permute-start | bytes 104456 | tf_op jit(solution)/shard_map/ppermute | solution.py:27
  12.4 6.0 %collective-permute-start.2 = (bf16[4,1,17,128]{3,2,1,0:T(8,128)(2,1)S(1)}, bf16[4,1,17,128]{3,2,1,0:T(8,128)(2,1)S(1)}, u32[]{:S(2)}, u32[]{:S(2)}) collective-permute-start(bf16[4,1,17,128]{3,2,1,0:T(8,128)(2,1)S(1)} %get-tuple-element.23), channel_id=1, source_target_pairs={{1,0},{2,1},{3,2},{5,4},{6,5},{7,6},{9,8},{10,9},{11,10},{13,12},{... | collective-permute-start | bytes 52232 | tf_op jit(solution)/shard_map/ppermute | solution.py:27
  13.7 4.9 %collective-permute-start.3 = (bf16[4,1,17,128]{3,2,1,0:T(8,128)(2,1)S(1)}, bf16[4,1,17,128]{3,2,1,0:T(8,128)(2,1)S(1)}, u32[]{:S(2)}, u32[]{:S(2)}) collective-permute-start(bf16[4,1,17,128]{3,2,1,0:T(8,128)(2,1)S(1)} %get-tuple-element.24), channel_id=1, source_target_pairs={{0,1},{1,2},{2,3},{4,5},{5,6},{6,7},{8,9},{9,10},{10,11},{12,13},{... | collective-permute-start | bytes 52232 | tf_op jit(solution)/shard_map/ppermute | solution.py:26
  19.5 1.0 copy-start.1
  20.6 6.0 %collective-permute-start.4 = (bf16[1,8,16,128]{3,2,1,0:T(8,128)(2,1)S(1)}, bf16[1,8,16,128]{3,2,1,0:T(8,128)(2,1)S(1)}, u32[]{:S(2)}, u32[]{:S(2)}) collective-permute-start(bf16[1,8,16,128]{3,2,1,0:T(8,128)(2,1)S(1)} %get-tuple-element.43), channel_id=1, source_target_pairs={{0,4},{4,8},{8,12},{12,16},{16,20},{20,24},{24,28},{1,5},{5,9},{9,... | collective-permute-start | bytes 98312 | tf_op jit(solution)/shard_map/ppermute | solution.py:26
  24.7 5.2 %collective-permute-start.5 = (bf16[1,8,16,128]{3,2,1,0:T(8,128)(2,1)S(1)}, bf16[1,8,16,128]{3,2,1,0:T(8,128)(2,1)S(1)}, u32[]{:S(2)}, u32[]{:S(2)}) collective-permute-start(bf16[1,8,16,128]{3,2,1,0:T(8,128)(2,1)S(1)} %get-tuple-element.44), channel_id=1, source_target_pairs={{4,0},{8,4},{12,8},{16,12},{20,16},{24,20},{28,24},{5,1},{9,5},{13... | collective-permute-start | bytes 98312 | tf_op jit(solution)/shard_map/ppermute | solution.py:27
  29.9 5.9 %collective-permute-start.6 = (bf16[4,1,16,128]{3,2,1,0:T(8,128)(2,1)S(1)}, bf16[4,1,16,128]{3,2,1,0:T(8,128)(2,1)S(1)}, u32[]{:S(2)}, u32[]{:S(2)}) collective-permute-start(bf16[4,1,16,128]{3,2,1,0:T(8,128)(2,1)S(1)} %get-tuple-element.35), channel_id=1, source_target_pairs={{1,0},{2,1},{3,2},{5,4},{6,5},{7,6},{9,8},{10,9},{11,10},{13,12},{... | collective-permute-start | bytes 49160 | tf_op jit(solution)/shard_map/ppermute | solution.py:27
  31.2 5.4 %collective-permute-start.7 = (bf16[4,1,16,128]{3,2,1,0:T(8,128)(2,1)S(1)}, bf16[4,1,16,128]{3,2,1,0:T(8,128)(2,1)S(1)}, u32[]{:S(2)}, u32[]{:S(2)}) collective-permute-start(bf16[4,1,16,128]{3,2,1,0:T(8,128)(2,1)S(1)} %get-tuple-element.36), channel_id=1, source_target_pairs={{0,1},{1,2},{2,3},{4,5},{5,6},{6,7},{8,9},{9,10},{10,11},{12,13},{... | collective-permute-start | bytes 49160 | tf_op jit(solution)/shard_map/ppermute | solution.py:26
  38.4 5.4 %collective-permute-start.8 = (bf16[1,8,16,128]{3,2,1,0:T(8,128)(2,1)S(1)}, bf16[1,8,16,128]{3,2,1,0:T(8,128)(2,1)S(1)}, u32[]{:S(2)}, u32[]{:S(2)}) collective-permute-start(bf16[1,8,16,128]{3,2,1,0:T(8,128)(2,1)S(1)} %get-tuple-element.41), channel_id=1, source_target_pairs={{0,4},{4,8},{8,12},{12,16},{16,20},{20,24},{24,28},{1,5},{5,9},{9,... | collective-permute-start | bytes 98312 | tf_op jit(solution)/shard_map/ppermute | solution.py:26
  41.2 5.2 %collective-permute-start.9 = (bf16[1,8,16,128]{3,2,1,0:T(8,128)(2,1)S(1)}, bf16[1,8,16,128]{3,2,1,0:T(8,128)(2,1)S(1)}, u32[]{:S(2)}, u32[]{:S(2)}) collective-permute-start(bf16[1,8,16,128]{3,2,1,0:T(8,128)(2,1)S(1)} %get-tuple-element.42), channel_id=1, source_target_pairs={{4,0},{8,4},{12,8},{16,12},{20,16},{24,20},{28,24},{5,1},{9,5},{13... | collective-permute-start | bytes 98312 | tf_op jit(solution)/shard_map/ppermute | solution.py:27
  46.4 5.8 %collective-permute-start.10 = (bf16[4,1,16,128]{3,2,1,0:T(8,128)(2,1)S(1)}, bf16[4,1,16,128]{3,2,1,0:T(8,128)(2,1)S(1)}, u32[]{:S(2)}, u32[]{:S(2)}) collective-permute-start(bf16[4,1,16,128]{3,2,1,0:T(8,128)(2,1)S(1)} %get-tuple-element.31), channel_id=1, source_target_pairs={{1,0},{2,1},{3,2},{5,4},{6,5},{7,6},{9,8},{10,9},{11,10},{13,12},{... | collective-permute-start | bytes 49160 | tf_op jit(solution)/shard_map/ppermute | solution.py:27
  47.7 5.4 %collective-permute-start.11 = (bf16[4,1,16,128]{3,2,1,0:T(8,128)(2,1)S(1)}, bf16[4,1,16,128]{3,2,1,0:T(8,128)(2,1)S(1)}, u32[]{:S(2)}, u32[]{:S(2)}) collective-permute-start(bf16[4,1,16,128]{3,2,1,0:T(8,128)(2,1)S(1)} %get-tuple-element.32), channel_id=1, source_target_pairs={{0,1},{1,2},{2,3},{4,5},{5,6},{6,7},{8,9},{9,10},{10,11},{12,13},{... | collective-permute-start | bytes 49160 | tf_op jit(solution)/shard_map/ppermute | solution.py:26
  53.9 15.0 %copy-start.2 = (f32[6,5]{1,0:T(8,128)S(1)}, f32[6,5]{1,0:T(8,128)}, u32[]{:S(2)}) copy-start(f32[6,5]{1,0:T(8,128)} %param.14) | copy-start | bytes 364
  54.9 6.3 %collective-permute-start.12 = (bf16[1,8,16,128]{3,2,1,0:T(8,128)(2,1)S(1)}, bf16[1,8,16,128]{3,2,1,0:T(8,128)(2,1)S(1)}, u32[]{:S(2)}, u32[]{:S(2)}) collective-permute-start(bf16[1,8,16,128]{3,2,1,0:T(8,128)(2,1)S(1)} %get-tuple-element.39), channel_id=1, source_target_pairs={{0,4},{4,8},{8,12},{12,16},{16,20},{20,24},{24,28},{1,5},{5,9},{9,... | collective-permute-start | bytes 98312 | tf_op jit(solution)/shard_map/ppermute | solution.py:26
  57.7 5.4 %collective-permute-start.13 = (bf16[1,8,16,128]{3,2,1,0:T(8,128)(2,1)S(1)}, bf16[1,8,16,128]{3,2,1,0:T(8,128)(2,1)S(1)}, u32[]{:S(2)}, u32[]{:S(2)}) collective-permute-start(bf16[1,8,16,128]{3,2,1,0:T(8,128)(2,1)S(1)} %get-tuple-element.40), channel_id=1, source_target_pairs={{4,0},{8,4},{12,8},{16,12},{20,16},{24,20},{28,24},{5,1},{9,5},{13... | collective-permute-start | bytes 98312 | tf_op jit(solution)/shard_map/ppermute | solution.py:27
  63.1 6.1 %collective-permute-start.14 = (bf16[4,1,16,128]{3,2,1,0:T(8,128)(2,1)S(1)}, bf16[4,1,16,128]{3,2,1,0:T(8,128)(2,1)S(1)}, u32[]{:S(2)}, u32[]{:S(2)}) collective-permute-start(bf16[4,1,16,128]{3,2,1,0:T(8,128)(2,1)S(1)} %get-tuple-element.27), channel_id=1, source_target_pairs={{1,0},{2,1},{3,2},{5,4},{6,5},{7,6},{9,8},{10,9},{11,10},{13,12},{... | collective-permute-start | bytes 49160 | tf_op jit(solution)/shard_map/ppermute | solution.py:27
  64.4 5.4 %collective-permute-start.15 = (bf16[4,1,16,128]{3,2,1,0:T(8,128)(2,1)S(1)}, bf16[4,1,16,128]{3,2,1,0:T(8,128)(2,1)S(1)}, u32[]{:S(2)}, u32[]{:S(2)}) collective-permute-start(bf16[4,1,16,128]{3,2,1,0:T(8,128)(2,1)S(1)} %get-tuple-element.28), channel_id=1, source_target_pairs={{0,1},{1,2},{2,3},{4,5},{5,6},{6,7},{8,9},{9,10},{10,11},{12,13},{... | collective-permute-start | bytes 49160 | tf_op jit(solution)/shard_map/ppermute | solution.py:26
